TPU v7x, 32 devices: a whole 2x2x4 slice. The times are simulated.
32 devices in a mesh: px: 4 (over z), py: 2 (over y), sa: 4 (over x, core).
Axes of the slice: x: 2, y: 2, z: 4, core: 2. Of those that a mesh axis runs over, the one named last changes fastest.
Arguments:
- real_coeffs: float32 [4, 256, 256, 256], P('sa', 'px', 'py'), may hold values from -6 to 6
- imaginary_coeffs: float32 [4, 256, 256, 256], P('sa', 'px', 'py'), may hold values from -6 to 6
Outputs:
- modulus: float32 [4, 256, 256, 256], P(None, ('px', 'py'), 'sa')
All inputs are finite; a program needn't handle non-finite values.
Results may differ from a plain program's by a relative error of at most 0.00007.
Values sent between devices are 32-bit elements; how exact they have to be, the bound alone decides.
No kernel may reach another device: no remote copies, remote signals or barrier semaphores. Data moves between devices by JAX's collectives and lax.ppermute only.
A program may use at most 128 MiB of HBM per device.

v0:
```python
from functools import partial
import math

import jax
import jax.numpy as jnp
from jax import lax
from jax.sharding import PartitionSpec as P

corr_length = 1.0
log_spread = 0.5


def matern(squared, length):
    return 1.0 / (1.0 + (2.0 * math.pi * corr_length / length) ** 2 * squared)


def matern_scale(length):
    middle = length // 2
    square_counts = {}
    for position in range(length):
        square_value = ((position + middle) % length - middle) ** 2
        square_counts[square_value] = square_counts.get(square_value, 0) + 1
    plane_counts = {}
    for first_square, first_count in square_counts.items():
        for second_square, second_count in square_counts.items():
            plane_sum = first_square + second_square
            plane_counts[plane_sum] = plane_counts.get(plane_sum, 0) + first_count * second_count
    running = 0.0
    for first_square, first_count in square_counts.items():
        for plane_sum, plane_count in plane_counts.items():
            running = (
                running + first_count * plane_count * matern(first_square + plane_sum, length) ** 2
            )
    return 1.0 / math.sqrt(running)


def signed(positions, length):
    return (positions + length // 2) % length - length // 2


def phase_tables(length, waves):
    positions = lax.iota(jnp.int32, length)
    phases = positions[:, None] * waves[None, :] % length
    angles = phases.astype(jnp.float32) * (2.0 * math.pi / length)
    return (jnp.cos(angles), jnp.sin(angles))


def transform(form, tables, pieces):
    cos_table, sin_table = tables
    real_in, imag_in = pieces
    product = partial(jnp.einsum, form, precision=lax.Precision.HIGHEST)
    real_out = product(cos_table, real_in) - product(sin_table, imag_in)
    imag_out = product(sin_table, real_in) + product(cos_table, imag_in)
    return (real_out, imag_out)


def finish(pieces, z_tables):
    cos_table, sin_table = z_tables
    product = partial(jnp.einsum, "zk,skxy->sxyz", precision=lax.Precision.HIGHEST)
    log_field = product(cos_table, pieces[0]) - product(sin_table, pieces[1])
    return jnp.exp(log_spread * log_field)


def z_phase_tables(length, rows_z, across_x, across_y):
    quarter = rows_z // across_x
    places = lax.iota(jnp.int32, length)
    sender = places // quarter
    z_waves = sender % across_y * rows_z + sender // across_y * quarter + places % quarter
    return phase_tables(length, z_waves)


def local(real_coeffs, imaginary_coeffs):
    length = real_coeffs.shape[3]
    rows_y = real_coeffs.shape[1]
    rows_z = real_coeffs.shape[2]
    across_x = lax.axis_size("px")
    across_y = lax.axis_size("py")
    freq_x = signed(lax.iota(jnp.int32, length), length).astype(jnp.float32)
    freq_y = signed(lax.iota(jnp.int32, rows_y) + lax.axis_index("px") * rows_y, length).astype(
        jnp.float32
    )
    freq_z = signed(lax.iota(jnp.int32, rows_z) + lax.axis_index("py") * rows_z, length).astype(
        jnp.float32
    )
    squared = freq_x[None, None, :] ** 2 + freq_y[:, None, None] ** 2 + freq_z[None, :, None] ** 2
    weight = matern(squared, length) * matern_scale(length)
    tables = phase_tables(length, lax.iota(jnp.int32, length))
    x_real, x_imag = transform(
        "xk,sabk->sabx", tables, (real_coeffs * weight, imaginary_coeffs * weight)
    )
    y_real, y_imag = transform(
        "yk,skqx->sqxy",
        tables,
        (
            lax.all_to_all(x_real, "px", split_axis=2, concat_axis=1, tiled=True),
            lax.all_to_all(x_imag, "px", split_axis=2, concat_axis=1, tiled=True),
        ),
    )
    z_tables = z_phase_tables(length, rows_z, across_x, across_y)
    local_field = finish(
        (
            lax.all_to_all(y_real, ("px", "py"), split_axis=2, concat_axis=1, tiled=True),
            lax.all_to_all(y_imag, ("px", "py"), split_axis=2, concat_axis=1, tiled=True),
        ),
        z_tables,
    )
    return lax.all_to_all(local_field, "sa", split_axis=2, concat_axis=0, tiled=True)


def solution(mesh):
    placed = (P("sa", "px", "py", None), P("sa", "px", "py", None))
    return jax.shard_map(
        local,
        mesh=mesh,
        in_specs=placed,
        out_specs=P(None, ("px", "py"), "sa", None),
        check_vma=False,
    )
```

profile of v0, /device:TPU:0, one launch (start us, length us, event | category | flops | bytes accessed | tf_op | source)
XLA Modules:
  0.0 1000.9 jit_solution(2427998826970052512)
XLA Ops:
  0.0 0.1 broadcast_add_fusion
  0.1 0.0 copy-start
  0.1 14.2 %fusion = f32[64,128,256]{2,1,0:T(8,128)} fusion(f32[1,64,128,256]{3,2,1,0:T(8,128)} %param.3, f32[128]{0:T(128)S(1)} %fusion.72, f32[64,256]{1,0:T(8,128)S(1)} %broadcast_add_fusion), kind=kOutput, calls=%fused_computation | convolution fusion | flops 6455951360 | bytes 16843264 | tf_op jit(solution)/shard_map/xk,sabk->sabx/dot_general | solution.py:53
  14.3 0.0 copy-done
  14.3 13.1 %add_bitcast_fusion.1 = f32[1,64,128,256]{3,2,1,0:T(8,128)S(1)} fusion(f32[64,128,256]{2,1,0:T(8,128)} %fusion, f32[1,64,128,256]{3,2,1,0:T(8,128)S(1)} %copy-done, f32[128]{0:T(128)S(1)} %fusion.72, f32[64,256]{1,0:T(8,128)S(1)} %broadcast_add_fusion), kind=kOutput, calls=%fused_computation.16 | convolution fusion | flops 6458048512 | bytes 25231872 | tf_op jit(solution)/shard_map/xk,sabk->sabx/dot_general | solution.py:53
  27.4 8.1 copy.35
  35.5 6.3 all-to-all-start.1
  41.9 12.9 %fusion.2 = f32[64,128,256]{2,1,0:T(8,128)S(1)} fusion(f32[1,64,128,256]{3,2,1,0:T(8,128)} %param.3, f32[128]{0:T(128)S(1)} %fusion.72, f32[64,256]{1,0:T(8,128)S(1)} %broadcast_add_fusion), kind=kOutput, calls=%fused_computation.2 | convolution fusion | flops 6455951360 | bytes 16843264 | tf_op jit(solution)/shard_map/xk,sabk->sabx/dot_general | solution.py:52
  54.7 13.1 %subtract_bitcast_fusion.1 = f32[1,64,128,256]{3,2,1,0:T(8,128)S(1)} fusion(f32[64,128,256]{2,1,0:T(8,128)S(1)} %fusion.2, f32[1,64,128,256]{3,2,1,0:T(8,128)} %param.2, f32[128]{0:T(128)S(1)} %fusion.72, f32[64,256]{1,0:T(8,128)S(1)} %broadcast_add_fusion), kind=kOutput, calls=%fused_computation.17 | convolution fusion | flops 6458048512 | bytes 25231872 | tf_op jit(solution)/shard_map/xk,sabk->sabx/dot_general | solution.py:52
  67.8 8.3 copy.31
  76.1 149.8 %all-to-all-done.1 = f32[1,64,128,256]{3,1,0,2:T(8,128)} async-done(((f32[1,64,128,256]{3,1,0,2:T(8,128)}), f32[1,64,128,256]{3,1,0,2:T(8,128)}, u32[]{:S(2)}, u32[]{:S(2)}) %all-to-all-start.1) | async-done | bytes 8388640 | tf_op jit(solution)/shard_map/all_to_all | solution.py:96
  225.9 5.7 all-to-all-start
  231.6 8.2 copy.36
  239.9 4.1 copy.37
  243.9 10.1 %copy.38 = f32[256,32,256]{0,2,1:T(8,128)} copy(f32[256,32,256]{2,1,0:T(8,128)} %bitcast.78) | data formatting | bytes 16777216 | tf_op jit(solution)/shard_map/reshape.12
  254.1 160.3 %all-to-all-done = f32[1,64,128,256]{3,1,0,2:T(8,128)} async-done(((f32[1,64,128,256]{3,1,0,2:T(8,128)}), f32[1,64,128,256]{3,1,0,2:T(8,128)}, u32[]{:S(2)}, u32[]{:S(2)}) %all-to-all-start) | async-done | bytes 8388640 | tf_op jit(solution)/shard_map/all_to_all | solution.py:95
  414.4 8.2 copy.32
  422.6 4.3 copy.33
  426.9 10.0 copy.34
  436.9 11.5 %fusion.35 = f32[32,256,256]{2,1,0:T(8,128)S(1)} fusion(f32[256,32,256]{0,2,1:T(8,128)} %copy.34), kind=kOutput, calls=%fused_computation.42 | convolution fusion | flops 6443368448 | bytes 16777216 | tf_op jit(solution)/shard_map/yk,skqx->sqxy/dot_general | solution.py:52
  448.4 11.6 %subtract_bitcast_fusion = f32[1,32,256,256]{3,2,1,0:T(8,128)S(1)} fusion(f32[32,256,256]{2,1,0:T(8,128)S(1)} %fusion.35, f32[256,32,256]{0,2,1:T(8,128)} %copy.38), kind=kOutput, calls=%fused_computation.15 | convolution fusion | flops 6445465600 | bytes 25165824 | tf_op jit(solution)/shard_map/yk,skqx->sqxy/dot_general | solution.py:52
  460.0 8.1 copy.39
  468.0 5.5 all-to-all-start.2
  473.5 11.1 %fusion.28 = f32[32,256,256]{2,1,0:T(8,128)S(1)} fusion(f32[256,32,256]{0,2,1:T(8,128)} %copy.34), kind=kOutput, calls=%fused_computation.35 | convolution fusion | flops 6443368448 | bytes 16777216 | tf_op jit(solution)/shard_map/yk,skqx->sqxy/dot_general | solution.py:53
  484.6 11.1 %add_bitcast_fusion = f32[1,32,256,256]{3,2,1,0:T(8,128)S(1)} fusion(f32[32,256,256]{2,1,0:T(8,128)S(1)} %fusion.28, f32[256,32,256]{0,2,1:T(8,128)} %copy.38), kind=kOutput, calls=%fused_computation.14 | convolution fusion | flops 6445465600 | bytes 25165824 | tf_op jit(solution)/shard_map/yk,skqx->sqxy/dot_general | solution.py:53
  495.7 8.3 copy.45
  503.9 152.2 %all-to-all-done.2 = f32[1,32,256,256]{3,1,0,2:T(8,128)} async-done(((f32[1,32,256,256]{3,1,0,2:T(8,128)}), f32[1,32,256,256]{3,1,0,2:T(8,128)}, u32[]{:S(2)}, u32[]{:S(2)}) %all-to-all-start.2) | async-done | bytes 8388640 | tf_op jit(solution)/shard_map/all_to_all | solution.py:102
  656.1 5.1 all-to-all-start.3
  661.3 8.2 copy.40
  669.5 4.1 copy.41
  673.6 169.5 %all-to-all-done.3 = f32[1,32,256,256]{3,1,0,2:T(8,128)} async-done(((f32[1,32,256,256]{3,1,0,2:T(8,128)}), f32[1,32,256,256]{3,1,0,2:T(8,128)}, u32[]{:S(2)}, u32[]{:S(2)}) %all-to-all-start.3) | async-done | bytes 8388640 | tf_op jit(solution)/shard_map/all_to_all | solution.py:103
  843.1 8.2 copy.46
  851.4 0.0 slice-start
  851.4 1.8 copy.47
  853.2 0.0 slice-start.1
  853.2 19.0 %fusion.8 = f32[32,256,256]{2,1,0:T(8,128)S(1)} fusion(f32[256,32,256]{2,1,0:T(8,128)S(1)} %bitcast.83, s32[256]{0:T(256)S(1)} %fusion.60), kind=kOutput, calls=%fused_computation.9 | convolution fusion | flops 6443368448 | bytes 16778240 | tf_op jit(solution)/shard_map/zk,skxy->sxyz/dot_general | solution.py:60
  872.3 0.0 slice-done
  872.3 0.0 slice-done.1
  872.3 19.4 %exponential_bitcast_fusion = f32[1,32,256,256]{3,2,1,0:T(8,128)S(1)} fusion(f32[32,256,256]{2,1,0:T(8,128)S(1)} %fusion.8, f32[256,32,256]{2,1,0:T(8,128)S(1)} %bitcast.76, s32[256]{0:T(256)S(1)} %fusion.60), kind=kOutput, calls=%fused_computation.13 | convolution fusion | flops 6447562752 | bytes 25166848 | tf_op jit(solution)/shard_map/zk,skxy->sxyz/dot_general | solution.py:60
  891.7 4.9 copy.49
  896.6 95.8 %all_to_all.78 = f32[1,32,256,256]{3,1,0,2:T(8,128)S(1)} all-to-all(f32[1,32,256,256]{3,1,0,2:T(8,128)S(1)} %copy.49), channel_id=1, replica_groups=mesh['px'=4,'py'=2,'sa'=4] {'sa'}, dimensions={2} | all-to-all | bytes 16777216 | tf_op jit(solution)/shard_map/all_to_all | solution.py:107
  992.4 8.3 copy.58
  (5 shorter events, 0.0 us)
Async XLA Ops:
  0.1 14.2 %copy-start = (f32[1,64,128,256]{3,2,1,0:T(8,128)S(1)}, f32[1,64,128,256]{3,2,1,0:T(8,128)}, u32[]{:S(2)}) copy-start(f32[1,64,128,256]{3,2,1,0:T(8,128)} %param.2) | copy-start | bytes 25165828
  35.5 190.4 %all-to-all-start.1 = ((f32[1,64,128,256]{3,1,0,2:T(8,128)}), f32[1,64,128,256]{3,1,0,2:T(8,128)}, u32[]{:S(2)}, u32[]{:S(2)}) async-start(f32[1,64,128,256]{3,1,0,2:T(8,128)} %copy.35), calls=%async_computation.1 | async-start | bytes 16777216 | tf_op jit(solution)/shard_map/all_to_all | solution.py:96
  225.9 188.5 %all-to-all-start = ((f32[1,64,128,256]{3,1,0,2:T(8,128)}), f32[1,64,128,256]{3,1,0,2:T(8,128)}, u32[]{:S(2)}, u32[]{:S(2)}) async-start(f32[1,64,128,256]{3,1,0,2:T(8,128)} %copy.31), calls=%async_computation | async-start | bytes 16777216 | tf_op jit(solution)/shard_map/all_to_all | solution.py:95
  468.0 188.1 %all-to-all-start.2 = ((f32[1,32,256,256]{3,1,0,2:T(8,128)}), f32[1,32,256,256]{3,1,0,2:T(8,128)}, u32[]{:S(2)}, u32[]{:S(2)}) async-start(f32[1,32,256,256]{3,1,0,2:T(8,128)} %copy.39), calls=%async_computation.2 | async-start | bytes 16777216 | tf_op jit(solution)/shard_map/all_to_all | solution.py:102
  656.1 187.0 %all-to-all-start.3 = ((f32[1,32,256,256]{3,1,0,2:T(8,128)}), f32[1,32,256,256]{3,1,0,2:T(8,128)}, u32[]{:S(2)}, u32[]{:S(2)}) async-start(f32[1,32,256,256]{3,1,0,2:T(8,128)} %copy.45), calls=%async_computation.3 | async-start | bytes 16777216 | tf_op jit(solution)/shard_map/all_to_all | solution.py:103
  851.4 20.9 %slice-start = ((s8[8388608]{0:T(1024)(128)(4,1)}), s8[4194304]{0:T(1024)(128)(4,1)S(1)}, s32[]{:S(2)}) async-start(s8[8388608]{0:T(1024)(128)(4,1)} %bitcast.74), calls=%async_computation.5 | async-start | bytes 8388608
  853.2 19.0 %slice-start.1 = ((s8[8388608]{0:T(1024)(128)(4,1)}), s8[4194304]{0:T(1024)(128)(4,1)S(1)}, s32[]{:S(2)}) async-start(s8[8388608]{0:T(1024)(128)(4,1)} %bitcast.74), calls=%async_computation.6 | async-start | bytes 8388608
where the time goes:
time: 1010 us; the launch traced here: 1000 us
  waiting for transfers between devices  632 us (63%)
  matrix products  137 us (14%)
  local copies, waits for them, and re-layouts  113 us (11%)
  blocking collectives  95.8 us (9%)
  starting transfers between devices  22.6 us (2%)
    all_to_all x1, waiting for transfers between devices, local(): lax.all_to_all(y_imag, ('px', 'py'), split_axis=2, concat_axis=1, tiled=T...  169 us
    all_to_all x1, waiting for transfers between devices, local(): lax.all_to_all(x_real, 'px', split_axis=2, concat_axis=1, tiled=True)  160 us
    all_to_all x1, waiting for transfers between devices, local(): lax.all_to_all(y_real, ('px', 'py'), split_axis=2, concat_axis=1, tiled=T...  152 us
    all_to_all x1, waiting for transfers between devices, local(): lax.all_to_all(x_imag, 'px', split_axis=2, concat_axis=1, tiled=True)  150 us
    all_to_all x1, blocking collectives, local(): lax.all_to_all(local_field, 'sa', split_axis=2, concat_axis=0, tiled=True)  95.8 us
    dot_general x4, matrix products, transform(): imag_out = product(sin_table, real_in) + product(cos_table, imag_in)  49.4 us
    dot_general x4, matrix products, transform(): real_out = product(cos_table, real_in) - product(sin_table, imag_in)  49.1 us
    dot_general x2, matrix products, finish(): log_field = product(cos_table, pieces[0]) - product(sin_table, pieces[1])  38.4 us
  transfers between devices with their start and end apart: 4, of which 4 were waited for; matrix products, arithmetic and copies ran while one was open for 10% of the time, Pallas kernels for 0%

commit v1 on v0

--- a/solution.py
+++ b/solution.py
@@ -38,9 +38,9 @@
     return (positions + length // 2) % length - length // 2
 
 
-def phase_tables(length, waves):
+def phase_tables(length):
     positions = lax.iota(jnp.int32, length)
-    phases = positions[:, None] * waves[None, :] % length
+    phases = positions[:, None] * positions[None, :] % length
     angles = phases.astype(jnp.float32) * (2.0 * math.pi / length)
     return (jnp.cos(angles), jnp.sin(angles))
 
@@ -54,25 +54,8 @@
     return (real_out, imag_out)
 
 
-def finish(pieces, z_tables):
-    cos_table, sin_table = z_tables
-    product = partial(jnp.einsum, "zk,skxy->sxyz", precision=lax.Precision.HIGHEST)
-    log_field = product(cos_table, pieces[0]) - product(sin_table, pieces[1])
-    return jnp.exp(log_spread * log_field)
-
-
-def z_phase_tables(length, rows_z, across_x, across_y):
-    quarter = rows_z // across_x
-    places = lax.iota(jnp.int32, length)
-    sender = places // quarter
-    z_waves = sender % across_y * rows_z + sender // across_y * quarter + places % quarter
-    return phase_tables(length, z_waves)
-
-
 def local(real_coeffs, imaginary_coeffs):
-    length = real_coeffs.shape[3]
-    rows_y = real_coeffs.shape[1]
-    rows_z = real_coeffs.shape[2]
+    samples, rows_y, rows_z, length = real_coeffs.shape
     across_x = lax.axis_size("px")
     across_y = lax.axis_size("py")
     freq_x = signed(lax.iota(jnp.int32, length), length).astype(jnp.float32)
@@ -84,27 +67,24 @@
     )
     squared = freq_x[None, None, :] ** 2 + freq_y[:, None, None] ** 2 + freq_z[None, :, None] ** 2
     weight = matern(squared, length) * matern_scale(length)
-    tables = phase_tables(length, lax.iota(jnp.int32, length))
-    x_real, x_imag = transform(
-        "xk,sabk->sabx", tables, (real_coeffs * weight, imaginary_coeffs * weight)
+    tables = phase_tables(length)
+    pieces = transform(
+        "xk,sabk->sxab", tables, (real_coeffs * weight, imaginary_coeffs * weight)
     )
-    y_real, y_imag = transform(
-        "yk,skqx->sqxy",
-        tables,
-        (
-            lax.all_to_all(x_real, "px", split_axis=2, concat_axis=1, tiled=True),
-            lax.all_to_all(x_imag, "px", split_axis=2, concat_axis=1, tiled=True),
-        ),
+
+    def gather(piece):
+        block = length // (across_x * across_y)
+        shaped = piece.reshape(samples, across_x * across_y, block, rows_y, rows_z)
+        moved = lax.all_to_all(shaped, ("px", "py"), split_axis=1, concat_axis=1, tiled=True)
+        parted = moved.reshape(samples, across_x, across_y, block, rows_y, rows_z)
+        return parted.transpose(0, 3, 1, 4, 2, 5).reshape(samples, block, length, length)
+
+    pieces = transform("yk,sxkq->sxyq", tables, tuple(gather(piece) for piece in pieces))
+    product = partial(jnp.einsum, "zk,sxyk->sxyz", precision=lax.Precision.HIGHEST)
+    log_field = product(tables[0], pieces[0]) - product(tables[1], pieces[1])
+    return lax.all_to_all(
+        jnp.exp(log_spread * log_field), "sa", split_axis=2, concat_axis=0, tiled=True
     )
-    z_tables = z_phase_tables(length, rows_z, across_x, across_y)
-    local_field = finish(
-        (
-            lax.all_to_all(y_real, ("px", "py"), split_axis=2, concat_axis=1, tiled=True),
-            lax.all_to_all(y_imag, ("px", "py"), split_axis=2, concat_axis=1, tiled=True),
-        ),
-        z_tables,
-    )
-    return lax.all_to_all(local_field, "sa", split_axis=2, concat_axis=0, tiled=True)
 
 
 def solution(mesh):

time: 1010 us -> 631 us (0.62)
  waiting for transfers between devices: 632 us -> 266 us
  local copies, waits for them, and re-layouts: 113 us -> 87.7 us
  matrix products: 137 us -> 159 us
    all_to_all x4 -> x2, waiting for transfers between devices: 632 us -> 266 us  [gather(): lax.all_to_all(shaped, ('px', 'py'), split_axis=1, concat_axis=1, tiled=T...]
    all_to_all x9 -> x1, local copies, waits for them, and re-layouts: 55.5 us -> 8.25 us  [local(): lax.all_to_all(jnp.exp(log_spread * log_field), 'sa', split_axis=2, conca...]
    reshape x0 -> x2, local copies, waits for them, and re-layouts: none -> 30.7 us  [gather(): parted = moved.reshape(samples, across_x, across_y, block, rows_y, rows_z)]
    dot_general x4, matrix products: 49.1 us -> 62.5 us  [transform(): real_out = product(cos_table, real_in) - product(sin_table, imag_in)]
    dot_general x4, matrix products: 49.4 us -> 61.5 us  [transform(): imag_out = product(sin_table, real_in) + product(cos_table, imag_in)]
    all_to_all x4 -> x2, starting transfers between devices: 22.6 us -> 13 us  [gather(): lax.all_to_all(shaped, ('px', 'py'), split_axis=1, concat_axis=1, tiled=T...]
  transfers between devices with their start and end apart: 4 -> 2, of which waited for: 4 -> 2; matrix products, arithmetic and copies ran while one was open for 10% -> 16% of each run, Pallas kernels for 0% -> 0%
where the time goes in v1:
time: 631 us; the launch traced here: 622 us
  waiting for transfers between devices  266 us (42%)
  matrix products  159 us (25%)
  blocking collectives  95.8 us (15%)
  local copies, waits for them, and re-layouts  87.7 us (14%)
  starting transfers between devices  13 us (2%)
    all_to_all x2, waiting for transfers between devices, gather(): lax.all_to_all(shaped, ('px', 'py'), split_axis=1, concat_axis=1, tiled=T...  266 us
    all_to_all x1, blocking collectives, local(): lax.all_to_all(jnp.exp(log_spread * log_field), 'sa', split_axis=2, conca...  95.8 us
    dot_general x4, matrix products, transform(): real_out = product(cos_table, real_in) - product(sin_table, imag_in)  62.5 us
    dot_general x4, matrix products, transform(): imag_out = product(sin_table, real_in) + product(cos_table, imag_in)  61.5 us
    dot_general x2, matrix products, local(): log_field = product(tables[0], pieces[0]) - product(tables[1], pieces[1])  35.4 us
    reshape x2, local copies, waits for them, and re-layouts, gather(): parted = moved.reshape(samples, across_x, across_y, block, rows_y, rows_z)  30.7 us
    another operation x2, local copies, waits for them, and re-layouts  23 us
    all_to_all x2, starting transfers between devices, gather(): lax.all_to_all(shaped, ('px', 'py'), split_axis=1, concat_axis=1, tiled=T...  13 us
  transfers between devices with their start and end apart: 2, of which 2 were waited for; matrix products, arithmetic and copies ran while one was open for 16% of the time, Pallas kernels for 0%

profile of v1, /device:TPU:0, one launch (start us, length us, event | category | flops | bytes accessed | tf_op | source)
XLA Modules:
  0.0 622.4 jit_solution(2009327160187105626)
XLA Ops:
  0.0 0.1 broadcast_add_fusion
  0.1 0.0 copy-start.2
  0.1 12.2 %fusion.4 = f32[64,128,256]{2,1,0:T(8,128)S(1)} fusion(f32[1,64,128,256]{3,2,1,0:T(8,128)} %param.3, f32[128]{0:T(128)S(1)} %fusion.63, f32[64,256]{1,0:T(8,128)S(1)} %broadcast_add_fusion), kind=kOutput, calls=%fused_computation.4 | convolution fusion | flops 6455951360 | bytes 16843264 | tf_op jit(solution)/shard_map/xk,sabk->sxab/dot_general | solution.py:53
  12.3 0.0 copy-done.2
  12.3 12.3 %add_bitcast_fusion = f32[1,256,64,128]{1,3,2,0:T(8,128)} fusion(f32[64,128,256]{2,1,0:T(8,128)S(1)} %fusion.4, f32[1,64,128,256]{3,2,1,0:T(8,128)S(1)} %copy-done.2, f32[128]{0:T(128)S(1)} %fusion.63, f32[64,256]{1,0:T(8,128)S(1)} %broadcast_add_fusion), kind=kOutput, calls=%fused_computation.18 | convolution fusion | flops 6458048512 | bytes 25231872 | tf_op jit(solution)/shard_map/xk,sabk->sxab/dot_general | solution.py:53
  24.6 8.7 %copy.23 = f32[1,256,64,128]{3,2,1,0:T(8,128)} copy(f32[1,256,64,128]{1,3,2,0:T(8,128)} %add_bitcast_fusion) | data formatting | bytes 16777216 | tf_op jit(solution)/shard_map/add | solution.py:53
  33.3 7.6 %all-to-all-start.1 = ((f32[1,8,32,64,128]{4,3,2,0,1:T(8,128)}), f32[1,8,32,64,128]{4,3,2,0,1:T(8,128)}, u32[]{:S(2)}, u32[]{:S(2)}) async-start(f32[1,8,32,64,128]{4,3,2,0,1:T(8,128)} %bitcast.89), calls=%async_computation.1 | async-start | bytes 16777216 | tf_op jit(solution)/shard_map/all_to_all | solution.py:78
  40.9 12.5 %fusion.6 = f32[64,128,256]{2,1,0:T(8,128)S(1)} fusion(f32[1,64,128,256]{3,2,1,0:T(8,128)} %param.3, f32[128]{0:T(128)S(1)} %fusion.63, f32[64,256]{1,0:T(8,128)S(1)} %broadcast_add_fusion), kind=kOutput, calls=%fused_computation.6 | convolution fusion | flops 6455951360 | bytes 16843264 | tf_op jit(solution)/shard_map/xk,sabk->sxab/dot_general | solution.py:52
  53.3 14.0 %subtract_bitcast_fusion = f32[1,256,64,128]{1,3,2,0:T(8,128)} fusion(f32[64,128,256]{2,1,0:T(8,128)S(1)} %fusion.6, f32[1,64,128,256]{3,2,1,0:T(8,128)} %param.2, f32[128]{0:T(128)S(1)} %fusion.63, f32[64,256]{1,0:T(8,128)S(1)} %broadcast_add_fusion), kind=kOutput, calls=%fused_computation.19 | convolution fusion | flops 6458048512 | bytes 25231872 | tf_op jit(solution)/shard_map/xk,sabk->sxab/dot_general | solution.py:52
  67.4 8.7 %copy.19 = f32[1,256,64,128]{3,2,1,0:T(8,128)} copy(f32[1,256,64,128]{1,3,2,0:T(8,128)} %subtract_bitcast_fusion) | data formatting | bytes 16777216 | tf_op jit(solution)/shard_map/sub | solution.py:52
  76.1 147.9 %all-to-all-done.1 = f32[1,8,32,64,128]{4,3,2,0,1:T(8,128)} async-done(((f32[1,8,32,64,128]{4,3,2,0,1:T(8,128)}), f32[1,8,32,64,128]{4,3,2,0,1:T(8,128)}, u32[]{:S(2)}, u32[]{:S(2)}) %all-to-all-start.1) | async-done | bytes 8388640 | tf_op jit(solution)/shard_map/all_to_all | solution.py:78
  224.0 5.4 all-to-all-start
  229.4 15.4 %copy.43 = f32[1,4,2,32,64,128]{5,2,4,1,3,0:T(2,128)} copy(f32[1,4,2,32,64,128]{5,4,3,2,1,0:T(8,128)} %bitcast.14) | data formatting | bytes 16777216 | tf_op jit(solution)/shard_map/reshape | solution.py:79
  244.8 11.5 %reshape.168 = f32[32,256,256]{2,1,0:T(8,128)} reshape(f32[1,32,4,64,2,128]{5,4,3,2,1,0:T(2,128)} %bitcast.90) | data formatting | bytes 16777216 | tf_op jit(solution)/shard_map/reshape.18
  256.3 0.0 copy-start
  256.3 19.4 %fusion.32 = f32[32,256,256]{2,1,0:T(8,128)} fusion(f32[32,256,256]{2,1,0:T(8,128)} %reshape.168), kind=kOutput, calls=%fused_computation.36 | convolution fusion | flops 6443368448 | bytes 16777216 | tf_op jit(solution)/shard_map/yk,sxkq->sxyq/dot_general | solution.py:53
  275.7 0.0 copy-done
  275.7 18.0 %fusion.28 = f32[32,256,256]{2,1,0:T(8,128)} fusion(f32[32,256,256]{2,1,0:T(8,128)S(1)} %copy-done), kind=kOutput, calls=%fused_computation.32 | convolution fusion | flops 6443368448 | bytes 16777216 | tf_op jit(solution)/shard_map/yk,sxkq->sxyq/dot_general | solution.py:52
  293.7 118.0 %all-to-all-done = f32[1,8,32,64,128]{4,3,2,0,1:T(8,128)} async-done(((f32[1,8,32,64,128]{4,3,2,0,1:T(8,128)}), f32[1,8,32,64,128]{4,3,2,0,1:T(8,128)}, u32[]{:S(2)}, u32[]{:S(2)}) %all-to-all-start) | async-done | bytes 8388640 | tf_op jit(solution)/shard_map/all_to_all | solution.py:78
  411.6 15.4 %copy.44 = f32[1,4,2,32,64,128]{5,2,4,1,3,0:T(2,128)} copy(f32[1,4,2,32,64,128]{5,4,3,2,1,0:T(8,128)} %bitcast.8) | data formatting | bytes 16777216 | tf_op jit(solution)/shard_map/reshape | solution.py:79
  427.0 11.5 %reshape.165 = f32[32,256,256]{2,1,0:T(8,128)} reshape(f32[1,32,4,64,2,128]{5,4,3,2,1,0:T(2,128)} %bitcast.91) | data formatting | bytes 16777216 | tf_op jit(solution)/shard_map/reshape.12
  438.5 0.0 copy-start.1
  438.5 0.0 slice-start
  438.5 17.6 %fusion.26 = f32[32,256,256]{2,1,0:T(8,128)S(1)} fusion(f32[32,256,256]{2,1,0:T(8,128)} %reshape.165), kind=kOutput, calls=%fused_computation.30 | convolution fusion | flops 6443368448 | bytes 16777216 | tf_op jit(solution)/shard_map/yk,sxkq->sxyq/dot_general | solution.py:53
  456.2 0.0 copy-done.1
  456.2 0.0 slice-start.1
  456.2 18.1 %fusion.36 = f32[32,256,256]{2,1,0:T(8,128)} fusion(f32[32,256,256]{2,1,0:T(8,128)S(1)} %copy-done.1), kind=kOutput, calls=%fused_computation.40 | convolution fusion | flops 6443368448 | bytes 16777216 | tf_op jit(solution)/shard_map/yk,sxkq->sxyq/dot_general | solution.py:52
  474.3 0.0 slice-done
  474.3 0.0 slice-done.1
  474.3 14.3 %fusion = f32[32,256,256]{2,1,0:T(8,128)S(1)} fusion(f32[32,256,256]{2,1,0:T(8,128)S(1)} %fusion.26, f32[32,256,256]{2,1,0:T(8,128)S(1)} %bitcast.87), kind=kOutput, calls=%fused_computation | convolution fusion | flops 6445465600 | bytes 25165824 | tf_op jit(solution)/shard_map/zk,sxyk->sxyz/dot_general | solution.py:84
  488.6 21.1 %exponential_bitcast_fusion = f32[1,32,256,256]{3,2,1,0:T(8,128)} fusion(f32[32,256,256]{2,1,0:T(8,128)S(1)} %fusion, f32[32,256,256]{2,1,0:T(8,128)} %fusion.36, f32[32,256,256]{2,1,0:T(8,128)} %fusion.28), kind=kOutput, calls=%fused_computation.15 | convolution fusion | flops 6449659904 | bytes 33554432 | tf_op jit(solution)/shard_map/zk,sxyk->sxyz/dot_general | solution.py:84
  509.7 8.2 %copy.31 = f32[1,32,256,256]{3,1,0,2:T(8,128)S(1)} copy(f32[1,32,256,256]{3,2,1,0:T(8,128)} %exponential_bitcast_fusion) | data formatting | bytes 16777216 | tf_op jit(solution)/shard_map/exp | solution.py:86
  517.9 95.8 %all_to_all.28 = f32[1,32,256,256]{3,1,0,2:T(8,128)S(1)} all-to-all(f32[1,32,256,256]{3,1,0,2:T(8,128)S(1)} %copy.31), channel_id=1, replica_groups=mesh['px'=4,'py'=2,'sa'=4] {'sa'}, dimensions={2} | all-to-all | bytes 16777216 | tf_op jit(solution)/shard_map/all_to_all | solution.py:85
  613.8 8.3 %copy.42 = f32[1,32,4,64,256]{4,3,1,2,0:T(8,128)} copy(f32[1,32,4,64,256]{4,1,3,2,0:T(8,128)S(1)} %bitcast.92) | data formatting | bytes 16777216 | tf_op jit(solution)/shard_map/all_to_all | solution.py:85
  (4 shorter events, 0.0 us)
Async XLA Ops:
  0.1 12.2 %copy-start.2 = (f32[1,64,128,256]{3,2,1,0:T(8,128)S(1)}, f32[1,64,128,256]{3,2,1,0:T(8,128)}, u32[]{:S(2)}) copy-start(f32[1,64,128,256]{3,2,1,0:T(8,128)} %param.2) | copy-start | bytes 25165828
  33.3 190.7 %all-to-all-start.1 = ((f32[1,8,32,64,128]{4,3,2,0,1:T(8,128)}), f32[1,8,32,64,128]{4,3,2,0,1:T(8,128)}, u32[]{:S(2)}, u32[]{:S(2)}) async-start(f32[1,8,32,64,128]{4,3,2,0,1:T(8,128)} %bitcast.89), calls=%async_computation.1 | async-start | bytes 16777216 | tf_op jit(solution)/shard_map/all_to_all | solution.py:78
  224.0 187.7 %all-to-all-start = ((f32[1,8,32,64,128]{4,3,2,0,1:T(8,128)}), f32[1,8,32,64,128]{4,3,2,0,1:T(8,128)}, u32[]{:S(2)}, u32[]{:S(2)}) async-start(f32[1,8,32,64,128]{4,3,2,0,1:T(8,128)} %bitcast.88), calls=%async_computation | async-start | bytes 16777216 | tf_op jit(solution)/shard_map/all_to_all | solution.py:78
  256.3 19.4 %copy-start = (f32[32,256,256]{2,1,0:T(8,128)S(1)}, f32[32,256,256]{2,1,0:T(8,128)}, u32[]{:S(2)}) copy-start(f32[32,256,256]{2,1,0:T(8,128)} %reshape.168) | copy-start | bytes 25165828
  438.5 17.6 %copy-start.1 = (f32[32,256,256]{2,1,0:T(8,128)S(1)}, f32[32,256,256]{2,1,0:T(8,128)}, u32[]{:S(2)}) copy-start(f32[32,256,256]{2,1,0:T(8,128)} %reshape.165) | copy-start | bytes 25165828
  438.5 35.7 %slice-start = ((s8[8388608]{0:T(1024)(128)(4,1)}), s8[4194304]{0:T(1024)(128)(4,1)S(1)}, s32[]{:S(2)}) async-start(s8[8388608]{0:T(1024)(128)(4,1)} %bitcast.86), calls=%async_computation.3 | async-start | bytes 8388608
  456.2 18.1 %slice-start.1 = ((s8[8388608]{0:T(1024)(128)(4,1)}), s8[4194304]{0:T(1024)(128)(4,1)S(1)}, s32[]{:S(2)}) async-start(s8[8388608]{0:T(1024)(128)(4,1)} %bitcast.86), calls=%async_computation.4 | async-start | bytes 8388608
